TPU v7x, 32 devices: a whole 2x2x4 slice. The times are simulated.
32 devices in a mesh: row: 4 (over y, x), col: 2 (over core), layer: 4 (over z).
Axes of the slice: x: 2, y: 2, z: 4, core: 2. Of those that a mesh axis runs over, the one named last changes fastest.
Arguments:
- matrix: float32 [4096, 4096], P('row', 'col'), may hold values from -6 to 6
- pattern: int32 [128, 128], P('row', 'col'), may hold values 0 or 1
- keep: int32 [128, 128], P('row', 'col'), may hold values 0 or 1
Outputs:
- update: float32 [4096, 4096], P(('row', 'layer'), 'col')
All inputs are finite; a program needn't handle non-finite values. No bound on the sum of `pattern` or of `keep` on one device may be relied on, other than what follows from the above.
Results may differ from a plain program's by a relative error of at most 0.00005.
Values sent between devices are 32-bit elements; how exact they have to be, the bound alone decides.
A program may use at most 128 MiB of HBM per device.

v0:
```python
import jax
import jax.numpy as jnp
from jax import lax
from jax.sharding import PartitionSpec as P

BS = 32
NB = 128


def layer_rows(values, layers, level):
    count, width = values.shape
    shaped = values.reshape(count // (layers * BS), layers, BS, width)
    picked = lax.dynamic_index_in_dim(shaped, level, 1, keepdims=False)
    return picked.reshape(count // layers, width)


def local(matrix, pattern, keep):
    rows, cols = matrix.shape
    block_rows, block_cols = pattern.shape
    layers = lax.axis_size("layer")
    level = lax.axis_index("layer")
    sparse = (
        matrix.reshape(block_rows, BS, block_cols, BS)
        * pattern.astype(jnp.float32)[:, None, :, None]
    ).reshape(rows, cols)
    left_local = lax.dynamic_index_in_dim(
        sparse.reshape(rows, block_cols // layers, layers, BS), level, 2, keepdims=False
    )
    left_local = left_local.reshape(rows, block_cols // layers * BS)
    left_full = lax.all_gather(left_local, "col", axis=1, tiled=True)
    right_full = lax.all_gather(layer_rows(sparse, layers, level), "row", axis=0, tiled=True)
    partial_value = jnp.dot(
        left_full, right_full, preferred_element_type=jnp.float32, precision=lax.Precision.HIGHEST
    )
    keep_flags = keep.astype(jnp.float32)
    keep_mine = lax.dynamic_index_in_dim(
        keep_flags.reshape(block_rows // layers, layers, block_cols), level, 1, keepdims=False
    )
    square = lax.psum(partial_value, "layer")
    mine = layer_rows(square, layers, level)
    filtered = (
        mine.reshape(block_rows // layers, BS, block_cols, BS) * keep_mine[:, None, :, None]
    ).reshape(rows // layers, cols)
    filtered_full = lax.all_gather(filtered, "row", axis=0, tiled=True)
    share = rows // layers
    summed = lax.psum_scatter(
        jnp.dot(
            left_full,
            filtered_full,
            preferred_element_type=jnp.float32,
            precision=lax.Precision.HIGHEST,
        ),
        "layer",
        scatter_dimension=0,
        tiled=True,
    )
    own_rows = lax.dynamic_slice_in_dim(sparse, level * share, share, 0)
    factor = 0.72 / (NB * BS)
    return 1.5 * own_rows - 0.5 * factor * summed


def solution(mesh):
    placed = (P("row", "col"), P("row", "col"), P("row", "col"))
    return jax.shard_map(
        local, mesh=mesh, in_specs=placed, out_specs=P(("row", "layer"), "col"), check_vma=False
    )
```

profile of v0, /device:TPU:0, one launch (start us, length us, event | category | flops | bytes accessed | tf_op | source)
XLA Modules:
  0.0 727.2 jit_solution(3081529053856967968)
XLA Ops:
  6.5 0.0 all-gather.4.cloned.1.call-start
  6.5 0.7 convert_element_type.6
  7.3 9.3 %copy.4 = f32[1024,2048]{0,1:T(8,128)} copy(f32[1024,2048]{1,0:T(8,128)} %param.3) | data formatting | bytes 16777216 | tf_op args[0]
  16.5 0.1 copy.5
  16.6 0.3 mul.63
  16.9 0.5 mul.64
  17.4 0.1 constant_dynamic-slice_fusion.3
  17.5 3.3 dynamic-slice_multiply_fusion.1
  20.8 0.0 all-gather.4.cloned.1.call-update
  20.8 0.0 all-gather.6.cloned.1.call-start
  20.9 0.3 mul.67
  21.2 0.5 mul.68
  21.7 0.1 constant_dynamic-slice_fusion.2
  21.8 3.2 dynamic-slice_multiply_fusion
  25.0 0.0 all-gather.6.cloned.1.call-update
  25.0 0.0 all-reduce.2.cloned.1.call-start
  25.1 12.3 %all-gather.4.cloned.1.call-done = f32[1024,1024]{0,1:T(8,128)} async-done(((f32[1024,512]{0,1:T(8,128)}), f32[1024,1024]{0,1:T(8,128)}) %all-gather.4.cloned.1.call-update) | async-done | bytes 4194320 | tf_op jit(solution)/shard_map/all_gather | solution.py:30
  37.4 90.5 %all-gather.6.cloned.1.call-done = f32[1024,2048]{1,0:T(8,128)} async-done(((f32[256,2048]{1,0:T(8,128)}), f32[1024,2048]{1,0:T(8,128)}) %all-gather.6.cloned.1.call-update) | async-done | bytes 8388624 | tf_op jit(solution)/shard_map/all_gather | solution.py:31
  127.9 31.0 %fusion.2 = f32[1024,2048]{1,0:T(8,128)} fusion(f32[1024,1024]{0,1:T(8,128)} %all-gather.4.cloned.1.call-done, f32[1024,2048]{1,0:T(8,128)} %all-gather.6.cloned.1.call-done), kind=kOutput, calls=%fused_computation.10 | convolution fusion | flops 25769803776 | bytes 20971520 | tf_op jit(solution)/shard_map/dot_general | solution.py:32
  158.9 0.0 copy-start
  158.9 0.0 all-reduce.2.cloned.1.call-update
  159.0 0.0 all-gather.8.cloned.1.call-start
  159.0 0.6 copy-done
  159.7 4.4 mul.72
  164.0 6.9 mul.73
  170.9 279.0 %all-reduce.2.cloned.1.call-done = f32[8,4,32,2048]{3,2,1,0:T(8,128)} async-done(((f32[8,4,32,2048]{3,2,1,0:T(8,128)}), f32[8,4,32,2048]{3,2,1,0:T(8,128)}) %all-reduce.2.cloned.1.call-update) | async-done | bytes 8388624 | tf_op jit(solution)/shard_map/psum | solution.py:39
  449.9 1.7 constant_dynamic-slice_fusion.1
  451.7 1.6 bitcast_multiply_fusion
  453.3 0.0 all-gather.8.cloned.1.call-update
  453.3 0.2 reduce-scatter.2.cloned.1.call-start
  453.5 86.4 %all-gather.8.cloned.1.call-done = f32[1024,2048]{1,0:T(8,128)} async-done(((f32[256,2048]{1,0:T(8,128)}), f32[1024,2048]{1,0:T(8,128)}) %all-gather.8.cloned.1.call-update) | async-done | bytes 8388624 | tf_op jit(solution)/shard_map/all_gather | solution.py:44
  539.9 31.0 %fusion.3 = f32[1024,2048]{1,0:T(8,128)} fusion(f32[1024,1024]{0,1:T(8,128)} %all-gather.4.cloned.1.call-done, f32[1024,2048]{1,0:T(8,128)} %all-gather.8.cloned.1.call-done), kind=kOutput, calls=%fused_computation.11 | convolution fusion | flops 25769803776 | bytes 20971520 | tf_op jit(solution)/shard_map/dot_general | solution.py:47
  571.0 0.0 reduce-scatter.2.cloned.1.call-update
  571.0 11.7 %mul.57 = f32[32,32,64,32]{3,2,1,0:T(8,128)} broadcast(f32[32,64]{1,0:T(8,128)S(1)} %convert_element_type.6), dimensions={0,2} | broadcast | bytes 8396800 | tf_op jit(solution)/shard_map/mul | solution.py:23
  582.6 25.5 %mul.58 = f32[1024,2048]{1,0:T(8,128)} reshape(f32[32,32,64,32]{3,2,1,0:T(8,128)} %mul.57) | data formatting | bytes 16777216 | tf_op jit(solution)/shard_map/mul | solution.py:23
  608.1 107.7 %reduce-scatter.2.cloned.1.call-done = f32[256,2048]{1,0:T(8,128)} async-done(((f32[1024,2048]{1,0:T(8,128)}), f32[256,2048]{1,0:T(8,128)}) %reduce-scatter.2.cloned.1.call-update) | async-done | bytes 2097168 | tf_op jit(solution)/shard_map/reduce_scatter | solution.py:46
  715.7 5.0 fusion.1
  (2 shorter events, 0.0 us)
Async XLA Ops:
  6.5 30.8 %all-gather.4.cloned.1.call-start = ((), (), s32[]{:S(2)}) async-start(), calls=%async_computation.1 | async-start | bytes 6291456 | tf_op jit(solution)/shard_map/all_gather | solution.py:30
  20.8 107.1 %all-gather.6.cloned.1.call-start = ((), (), s32[]{:S(2)}) async-start(), calls=%async_computation.2 | async-start | bytes 10485760 | tf_op jit(solution)/shard_map/all_gather | solution.py:31
  25.0 424.9 %all-reduce.2.cloned.1.call-start = ((), (), s32[]{:S(2)}) async-start(), calls=%async_computation.3 | async-start | bytes 16777216 | tf_op jit(solution)/shard_map/psum | solution.py:39
  158.9 0.7 copy-start
  159.0 381.0 %all-gather.8.cloned.1.call-start = ((), (), s32[]{:S(2)}) async-start(), calls=%async_computation.4 | async-start | bytes 10485760 | tf_op jit(solution)/shard_map/all_gather | solution.py:44
  453.3 262.4 %reduce-scatter.2.cloned.1.call-start = ((), (), s32[]{:S(2)}) async-start(), calls=%async_computation.5 | async-start | bytes 10485760 | tf_op jit(solution)/shard_map/reduce_scatter | solution.py:46
Sparse Core Ops, SparseCore 0:
  20.9 16.3 all-gather.3
  39.2 88.6 all-gather.5
  159.1 290.8 all-reduce.1
  453.4 86.4 all-gather.7
  571.1 144.6 reduce-scatter.1
where the time goes:
time: 728 us; the launch traced here: 727 us
  waiting for transfers between devices  576 us (79%)
  matrix products  62.1 us (9%)
  local copies, waits for them, and re-layouts  61.9 us (9%)
  other arithmetic  13.8 us (2%)
  between operations  13.2 us (2%)
    psum x1, waiting for transfers between devices, local(): square = lax.psum(partial_value, 'layer')  279 us
    reduce_scatter x1, waiting for transfers between devices, local(): lax.psum_scatter(jnp.dot(left_full, filtered_full, preferred_element_type...  108 us
    all_gather x1, waiting for transfers between devices, local(): lax.all_gather(layer_rows(sparse, layers, level), 'row', axis=0, tiled=True)  90.5 us
    all_gather x1, waiting for transfers between devices, local(): filtered_full = lax.all_gather(filtered, 'row', axis=0, tiled=True)  86.4 us
    mul x6, local copies, waits for them, and re-layouts, local(): matrix.reshape(block_rows, BS, block_cols, BS)  38.8 us
    dot_general x1, matrix products, local(): jnp.dot(left_full, right_full, preferred_element_type=jnp.float32, precis...  31 us
    dot_general x1, matrix products, local(): jnp.dot(left_full, filtered_full, preferred_element_type=jnp.float32, pre...  31 us
  transfers between devices with their start and end apart: 5, of which 5 were waited for; matrix products, arithmetic and copies ran while one was open for 7% of the time, Pallas kernels for 0%

commit v1 on v0

--- a/solution.py
+++ b/solution.py
@@ -5,6 +5,14 @@
 
 BS = 32
 NB = 128
+
+
+def add_in_pairs(block, name):
+    count, total = (lax.axis_size(name), block)
+    for far in [1 << k for k in range(count.bit_length() - 1)]:
+        pairs = [(i, i ^ far) for i in range(count)]
+        total = total + lax.ppermute(total, name, pairs)
+    return total
 
 
 def layer_rows(values, layers, level):
@@ -36,7 +44,7 @@
     keep_mine = lax.dynamic_index_in_dim(
         keep_flags.reshape(block_rows // layers, layers, block_cols), level, 1, keepdims=False
     )
-    square = lax.psum(partial_value, "layer")
+    square = add_in_pairs(partial_value, "layer")
     mine = layer_rows(square, layers, level)
     filtered = (
         mine.reshape(block_rows // layers, BS, block_cols, BS) * keep_mine[:, None, :, None]

time: 728 us -> 1010 us (1.39)
  waiting for transfers between devices: 576 us -> 827 us
  other arithmetic: 13.8 us -> 37.2 us
    ppermute x0 -> x2, waiting for transfers between devices: none -> 529 us  [add_in_pairs(): total = total + lax.ppermute(total, name, pairs)]
    psum x1 -> x0, waiting for transfers between devices: 279 us -> none  [local(): square = lax.psum(partial_value, 'layer')]
    add x0 -> x2, other arithmetic: none -> 23.4 us  [add_in_pairs(): total = total + lax.ppermute(total, name, pairs)]
  transfers between devices with their start and end apart: 5 -> 6, of which waited for: 5 -> 6; matrix products, arithmetic and copies ran while one was open for 7% -> 5% of each run, Pallas kernels for 0% -> 0%
where the time goes in v1:
time: 1010 us
  waiting for transfers between devices  827 us (82%)
  local copies, waits for them, and re-layouts  64.2 us (6%)
  matrix products  60.7 us (6%)
  other arithmetic  37.2 us (4%)
  between operations  13.2 us (1%)
    ppermute x2, waiting for transfers between devices, add_in_pairs(): total = total + lax.ppermute(total, name, pairs)  529 us
    reduce_scatter x1, waiting for transfers between devices, local(): lax.psum_scatter(jnp.dot(left_full, filtered_full, preferred_element_type...  108 us
    all_gather x1, waiting for transfers between devices, local(): lax.all_gather(layer_rows(sparse, layers, level), 'row', axis=0, tiled=True)  90.5 us
    all_gather x1, waiting for transfers between devices, local(): filtered_full = lax.all_gather(filtered, 'row', axis=0, tiled=True)  87.6 us
    mul x6, local copies, waits for them, and re-layouts, local(): matrix.reshape(block_rows, BS, block_cols, BS)  38.7 us
    dot_general x1, matrix products, local(): jnp.dot(left_full, filtered_full, preferred_element_type=jnp.float32, pre...  31 us
    dot_general x1, matrix products, local(): jnp.dot(left_full, right_full, preferred_element_type=jnp.float32, precis...  29.7 us
    add x2, other arithmetic, add_in_pairs(): total = total + lax.ppermute(total, name, pairs)  23.4 us
  transfers between devices with their start and end apart: 6, of which 6 were waited for; matrix products, arithmetic and copies ran while one was open for 5% of the time, Pallas kernels for 0%

profile of v1, /device:TPU:0, one launch (start us, length us, event | category | flops | bytes accessed | tf_op | source)
XLA Modules:
  0.0 1006.8 jit_solution(2441784847759672998)
XLA Ops:
  6.5 0.0 all-gather.4.cloned.1.call-start
  6.5 0.7 convert_element_type.6
  7.3 9.3 copy.4
  16.5 0.1 copy.5
  16.6 0.3 mul.63
  16.9 0.5 mul.64
  17.4 0.1 constant_dynamic-slice_fusion.3
  17.5 3.3 dynamic-slice_multiply_fusion.1
  20.8 0.0 all-gather.4.cloned.1.call-update
  20.8 0.0 all-gather.6.cloned.1.call-start
  20.9 0.3 mul.67
  21.2 0.5 mul.68
  21.7 0.1 constant_dynamic-slice_fusion.2
  21.8 3.3 dynamic-slice_multiply_fusion
  25.0 0.0 all-gather.6.cloned.1.call-update
  25.1 0.2 all-gather.8.cloned.1.call-start
  25.3 12.1 %all-gather.4.cloned.1.call-done = f32[1024,1024]{0,1:T(8,128)} async-done(((f32[1024,512]{0,1:T(8,128)}), f32[1024,1024]{0,1:T(8,128)}) %all-gather.4.cloned.1.call-update) | async-done | bytes 4194320 | tf_op jit(solution)/shard_map/all_gather | solution.py:38
  37.4 90.5 %all-gather.6.cloned.1.call-done = f32[1024,2048]{1,0:T(8,128)} async-done(((f32[256,2048]{1,0:T(8,128)}), f32[1024,2048]{1,0:T(8,128)}) %all-gather.6.cloned.1.call-update) | async-done | bytes 8388624 | tf_op jit(solution)/shard_map/all_gather | solution.py:39
  127.9 29.7 %fusion.2 = f32[1024,2048]{1,0:T(8,128)S(1)} fusion(f32[1024,1024]{0,1:T(8,128)} %all-gather.4.cloned.1.call-done, f32[1024,2048]{1,0:T(8,128)} %all-gather.6.cloned.1.call-done), kind=kOutput, calls=%fused_computation.10 | convolution fusion | flops 25769803776 | bytes 20971520 | tf_op jit(solution)/shard_map/dot_general | solution.py:40
  157.6 0.0 copy-start
  157.6 3.2 copy-done
  160.8 0.0 copy-start.1
  160.8 1.5 collective-permute-start
  162.3 180.7 %collective-permute-done = f32[1024,2048]{1,0:T(8,128)} collective-permute-done((f32[1024,2048]{1,0:T(8,128)S(1)}, f32[1024,2048]{1,0:T(8,128)}, u32[]{:S(2)}, u32[]{:S(2)}) %collective-permute-start) | collective-permute-done | bytes 8388640 | tf_op jit(solution)/shard_map/ppermute | solution.py:14
  342.9 11.7 %add.22 = f32[1024,2048]{1,0:T(8,128)} add(f32[1024,2048]{1,0:T(8,128)} %copy-done, f32[1024,2048]{1,0:T(8,128)} %collective-permute-done) | non-fusion elementwise | flops 2097152 | bytes 25165824 | tf_op jit(solution)/shard_map/add | solution.py:14
  354.6 2.4 collective-permute-start.1
  357.0 0.0 copy-done.1
  357.1 4.4 mul.72
  361.4 6.7 mul.73
  368.1 348.7 %collective-permute-done.1 = f32[1024,2048]{1,0:T(8,128)} collective-permute-done((f32[1024,2048]{1,0:T(8,128)}, f32[1024,2048]{1,0:T(8,128)}, u32[]{:S(2)}, u32[]{:S(2)}) %collective-permute-start.1) | collective-permute-done | bytes 8388640 | tf_op jit(solution)/shard_map/ppermute | solution.py:14
  716.8 11.7 %add.23 = f32[1024,2048]{1,0:T(8,128)} add(f32[1024,2048]{1,0:T(8,128)} %add.22, f32[1024,2048]{1,0:T(8,128)} %collective-permute-done.1) | non-fusion elementwise | flops 2097152 | bytes 25165824 | tf_op jit(solution)/shard_map/add | solution.py:14
  728.5 1.7 constant_dynamic-slice_fusion.1
  730.2 1.6 bitcast_multiply_fusion
  731.9 0.0 all-gather.8.cloned.1.call-update
  731.9 0.0 reduce-scatter.2.cloned.1.call-start
  731.9 87.6 %all-gather.8.cloned.1.call-done = f32[1024,2048]{1,0:T(8,128)} async-done(((f32[256,2048]{1,0:T(8,128)}), f32[1024,2048]{1,0:T(8,128)}) %all-gather.8.cloned.1.call-update) | async-done | bytes 8388624 | tf_op jit(solution)/shard_map/all_gather | solution.py:52
  819.5 31.0 %fusion.3 = f32[1024,2048]{1,0:T(8,128)} fusion(f32[1024,1024]{0,1:T(8,128)} %all-gather.4.cloned.1.call-done, f32[1024,2048]{1,0:T(8,128)} %all-gather.8.cloned.1.call-done), kind=kOutput, calls=%fused_computation.11 | convolution fusion | flops 25769803776 | bytes 20971520 | tf_op jit(solution)/shard_map/dot_general | solution.py:55
  850.5 0.0 reduce-scatter.2.cloned.1.call-update
  850.5 11.7 %mul.57 = f32[32,32,64,32]{3,2,1,0:T(8,128)} broadcast(f32[32,64]{1,0:T(8,128)S(1)} %convert_element_type.6), dimensions={0,2} | broadcast | bytes 8396800 | tf_op jit(solution)/shard_map/mul | solution.py:31
  862.2 25.4 %mul.58 = f32[1024,2048]{1,0:T(8,128)} reshape(f32[32,32,64,32]{3,2,1,0:T(8,128)} %mul.57) | data formatting | bytes 16777216 | tf_op jit(solution)/shard_map/mul | solution.py:31
  887.6 107.7 %reduce-scatter.2.cloned.1.call-done = f32[256,2048]{1,0:T(8,128)} async-done(((f32[1024,2048]{1,0:T(8,128)}), f32[256,2048]{1,0:T(8,128)}) %reduce-scatter.2.cloned.1.call-update) | async-done | bytes 2097168 | tf_op jit(solution)/shard_map/reduce_scatter | solution.py:54
  995.3 5.0 fusion.1
  (2 shorter events, 0.0 us)
Async XLA Ops:
  6.5 30.8 %all-gather.4.cloned.1.call-start = ((), (), s32[]{:S(2)}) async-start(), calls=%async_computation.1 | async-start | bytes 6291456 | tf_op jit(solution)/shard_map/all_gather | solution.py:38
  20.8 107.1 %all-gather.6.cloned.1.call-start = ((), (), s32[]{:S(2)}) async-start(), calls=%async_computation.2 | async-start | bytes 10485760 | tf_op jit(solution)/shard_map/all_gather | solution.py:39
  25.1 794.4 %all-gather.8.cloned.1.call-start = ((), (), s32[]{:S(2)}) async-start(), calls=%async_computation.3 | async-start | bytes 10485760 | tf_op jit(solution)/shard_map/all_gather | solution.py:52
  157.6 3.2 copy-start
  160.8 196.2 %copy-start.1 = (s32[32,64]{1,0:T(8,128)S(1)}, s32[32,64]{1,0:T(8,128)}, u32[]{:S(2)}) copy-start(s32[32,64]{1,0:T(8,128)} %param.5) | copy-start | bytes 24580
  160.8 182.1 %collective-permute-start = (f32[1024,2048]{1,0:T(8,128)S(1)}, f32[1024,2048]{1,0:T(8,128)}, u32[]{:S(2)}, u32[]{:S(2)}) collective-permute-start(f32[1024,2048]{1,0:T(8,128)S(1)} %fusion.2), channel_id=1, source_target_pairs={{0,1},{1,0},{2,3},{3,2},{4,5},{5,4},{6,7},{7,6},{8,9},{9,8},{10,11... | collective-permute-start | bytes 25165832 | tf_op jit(solution)/shard_map/ppermute | solution.py:14
  354.6 362.1 %collective-permute-start.1 = (f32[1024,2048]{1,0:T(8,128)}, f32[1024,2048]{1,0:T(8,128)}, u32[]{:S(2)}, u32[]{:S(2)}) collective-permute-start(f32[1024,2048]{1,0:T(8,128)} %add.22), channel_id=1, source_target_pairs={{0,2},{1,3},{2,0},{3,1},{4,6},{5,7},{6,4},{7,5},{8,10},{9,11},{10,... | collective-permute-start | bytes 25165832 | tf_op jit(solution)/shard_map/ppermute | solution.py:14
  731.9 263.4 %reduce-scatter.2.cloned.1.call-start = ((), (), s32[]{:S(2)}) async-start(), calls=%async_computation.4 | async-start | bytes 10485760 | tf_op jit(solution)/shard_map/reduce_scatter | solution.py:54
Sparse Core Ops, SparseCore 0:
  20.9 16.3 all-gather.3
  39.2 88.6 all-gather.5
  732.0 87.4 all-gather.7
  850.7 144.6 reduce-scatter.1
